TPU v7x, 32 devices: a whole 2x2x4 slice. The times are simulated.
32 devices in a mesh: groups: 2 (over x), space: 16 (over z, y, core).
Axes of the slice: x: 2, y: 2, z: 4, core: 2. Of those that a mesh axis runs over, the one named last changes fastest.
Arguments:
- hidden: bfloat16 [4096, 512], P(('groups', 'space')), parts along dimension 0, may hold values from -130 to 130
- norm_gain: float32 [512], replicated, may hold values from 0.5 to 2
- norm_shift: float32 [512], replicated, may hold values from -3 to 3
- conv_weight: bfloat16 [3, 3, 3, 512, 512], P(None, None, None, 'space'), may hold values from -0.0546875 to 0.0546875
- conv_bias: bfloat16 [512], replicated, may hold values from -3 to 3
Outputs:
- decoded: bfloat16 [8, 32, 64, 512], P('groups', None, 'space'), parts along dimension 0
There are 2 independent parts, one for each index of `groups`. A program takes and returns all parts, laid end to end along the dimension named above; an argument that names none is the same for every part. Nothing has to cross between parts.
All inputs are finite; a program needn't handle non-finite values.
Results may differ from a plain program's by a relative error of at most 0.0045.
Values may be sent and summed in bfloat16 or wider, within the bound.
A program may use at most 64 MiB of HBM per device.

v0:
```python
import jax
import jax.numpy as jnp
from jax import lax
from jax.sharding import PartitionSpec as P

CHANNELS = 512
GROUPS = 32
FRAMES = 4
ROWS = 16
COL_DEV = 2


EPSILON = 1e-06


def with_halo(x, sides, width):
    for axis, dim in sides:
        size, length = (lax.axis_size(axis), x.shape[dim])
        up = [(i, (i + 1) % size) for i in range(size - 1)]
        down = [(j, i) for i, j in up]
        last = lax.slice_in_dim(x, length - width, length, axis=dim)
        first = lax.slice_in_dim(x, 0, width, axis=dim)
        before = lax.ppermute(last, axis, up)
        after = lax.ppermute(first, axis, down)
        x = jnp.concatenate([before, x, after], axis=dim)
    return x


def group_moments(values, population):
    grouped = values.reshape(-1, GROUPS, CHANNELS // GROUPS).astype(jnp.float32)
    totals, squares = lax.psum(
        (jnp.sum(grouped, axis=(0, 2)), jnp.sum(grouped * grouped, axis=(0, 2))), "space"
    )
    average = totals / population
    spread = squares / population - average * average
    return (average, spread)


def shards(hidden, norm_gain, norm_shift, conv_weight, conv_bias):
    devices = lax.axis_size("space")
    rows_dev = hidden.shape[0] // (COL_DEV * devices)
    population = float(FRAMES * ROWS * COL_DEV * devices * (CHANNELS // GROUPS))
    layout = hidden.reshape(rows_dev, devices * COL_DEV, CHANNELS)
    tile_cells = lax.all_to_all(layout, "space", split_axis=1, concat_axis=0, tiled=True)
    average, spread = group_moments(tile_cells, population)
    scaled = tile_cells.astype(jnp.float32).reshape(
        FRAMES, ROWS, COL_DEV, GROUPS, CHANNELS // GROUPS
    )
    scaled = (scaled - average[:, None]) * lax.rsqrt(spread + EPSILON)[:, None]
    normed = scaled.reshape(FRAMES, ROWS, COL_DEV, CHANNELS) * norm_gain + norm_shift
    active = jax.nn.silu(normed).astype(jnp.bfloat16)
    widened = with_halo(active, (("space", 2),), 1)
    position = lax.axis_index("space")
    lefthand = jnp.where(position == 0, active[:, :, :1], widened[:, :, :1])
    righthand = jnp.where(position == devices - 1, active[:, :, -1:], widened[:, :, -1:])
    widened = jnp.concatenate([lefthand, active, righthand], axis=2)
    doubled = jnp.repeat(jnp.repeat(widened, 2, axis=1), 2, axis=2)[:, :, 1:-1]
    padded = jnp.pad(doubled, ((2, 0), (1, 1), (0, 0), (0, 0)), mode="edge")
    initial = jnp.zeros((FRAMES, 2 * ROWS, 2 * COL_DEV, CHANNELS), jnp.float32)
    product = lax.conv_general_dilated(
        padded[None],
        lax.all_gather(conv_weight, "space", axis=3, tiled=True),
        (1, 1, 1),
        "VALID",
        dimension_numbers=("NDHWC", "DHWIO", "NDHWC"),
        preferred_element_type=jnp.float32,
    )
    summed = initial + product[0]
    return (summed + conv_bias.astype(jnp.float32)).astype(jnp.bfloat16)


def solution(mesh):
    placed = (P(("groups", "space"), None), P(), P(), P(None, None, None, "space", None), P())
    return jax.shard_map(
        shards,
        mesh=mesh,
        in_specs=placed,
        out_specs=P("groups", None, "space", None),
        check_vma=False,
    )
```

profile of v0, /device:TPU:0, one launch (start us, length us, event | category | flops | bytes accessed | tf_op | source)
XLA Modules:
  0.0 173.3 jit_solution(17205814348550977458)
XLA Ops:
  6.5 0.7 all-gather.2.cloned.1.call-update
  7.3 1.0 copy.12
  8.3 15.2 %all_to_all.4 = bf16[4,32,512]{2,0,1:T(4,128)(2,1)S(1)} all-to-all(bf16[4,32,512]{2,0,1:T(4,128)(2,1)S(1)} %copy.12), channel_id=1, replica_groups=mesh['groups'=2,'space'=16] {'space'}, dimensions={1} | all-to-all | bytes 262144 | tf_op jit(solution)/shard_map/all_to_all | solution.py:44
  23.5 0.1 convert_reduce_fusion
  23.6 0.1 reduce_sum.24
  23.7 0.1 reduce_sum.36
  23.8 0.1 reduce_sum.25
  23.9 0.1 reduce_sum.37
  24.0 32.3 %all-reduce = (f32[32]{0:T(128)S(1)}, f32[32]{0:T(128)S(1)}) all-reduce(f32[32]{0:T(128)S(1)} %reduce_sum.37, f32[32]{0:T(128)S(1)} %reduce_sum.25), channel_id=1, replica_groups=mesh['groups'=2,'space'=16] {'space'}, use_global_device_ids=true, to_apply=%region_5.6 | all-reduce | flops 64 | bytes 512 | tf_op jit(solution)/shard_map/psum | solution.py:31
  56.3 0.1 mul.36
  56.4 0.1 mul.37
  56.5 0.1 sub.17
  56.6 0.1 copy.13
  56.8 0.8 multiply_convert_fusion
  57.6 1.3 collective-permute-start
  58.9 1.3 collective-permute-start.1
  60.2 1.9 %collective-permute-done.1 = bf16[4,16,1,512]{3,1,2,0:T(8,128)(2,1)S(1)} collective-permute-done((bf16[4,16,1,512]{3,1,2,0:T(8,128)(2,1)S(1)}, bf16[4,16,1,512]{3,1,2,0:T(8,128)(2,1)S(1)}, u32[]{:S(2)}, u32[]{:S(2)}) %collective-permute-start.1) | collective-permute-done | bytes 65568 | tf_op jit(solution)/shard_map/ppermute | solution.py:24
  62.2 0.4 broadcast_in_dim.14
  62.7 0.2 reshape.36
  62.9 0.1 broadcast_in_dim.15
  63.1 0.6 fusion.9
  63.8 59.1 %all-gather.2.cloned.1.call-done = bf16[3,3,3,512,512]{4,3,2,1,0:T(8,128)(2,1)} async-done(((bf16[3,3,3,32,512]{4,3,2,1,0:T(8,128)(2,1)}), bf16[3,3,3,512,512]{4,3,2,1,0:T(8,128)(2,1)}) %all-gather.2.cloned.1.call-update) | async-done | bytes 14155792 | tf_op jit(solution)/shard_map/all_gather | solution.py:62
  122.8 42.6 %fusion.4 = f32[1,4,32,4,512]{4,0,3,2,1:T(1,128)S(1)} fusion(bf16[3,3,3,512,512]{4,3,2,1,0:T(8,128)(2,1)} %all-gather.2.cloned.1.call-done, bf16[1,6,34,6,512]{4,2,3,1,0:T(8,128)(2,1)S(1)} %fusion.9), kind=kOutput, calls=%fused_computation.6 | convolution fusion | flops 7247757312 | bytes 16457728 | tf_op jit(solution)/shard_map/conv_general_dilated | solution.py:60
  165.4 1.1 fusion.11
  (14 shorter events, 0.3 us)
Async XLA Ops:
  6.5 53.7 %copy-start = (bf16[512]{0:T(512)(128)(2,1)S(1)}, bf16[512]{0:T(512)(128)(2,1)}, u32[]{:S(2)}) copy-start(bf16[512]{0:T(512)(128)(2,1)} %param.9) | copy-start | bytes 3076
  6.5 116.3 %all-gather.2.cloned.1.call-start = ((), (), s32[]{:S(2)}) async-start(), calls=%async_computation.1 | async-start | bytes 15040512 | tf_op jit(solution)/shard_map/all_gather | solution.py:62
  57.6 2.6 %collective-permute-start = (bf16[4,16,1,512]{3,1,2,0:T(8,128)(2,1)S(1)}, bf16[4,16,1,512]{3,1,2,0:T(8,128)(2,1)S(1)}, u32[]{:S(2)}, u32[]{:S(2)}) collective-permute-start(bf16[4,16,1,512]{3,1,2,0:T(8,128)(2,1)S(1)} %get-tuple-element.11), channel_id=1, source_target_pairs={{0,1},{1,2},{2,3},{3,4},{4,5},{5,6},{6,7},{7,8},{8,9},{9,10},{10,1... | collective-permute-start | bytes 196616 | tf_op jit(solution)/shard_map/ppermute | solution.py:23
  58.9 3.3 %collective-permute-start.1 = (bf16[4,16,1,512]{3,1,2,0:T(8,128)(2,1)S(1)}, bf16[4,16,1,512]{3,1,2,0:T(8,128)(2,1)S(1)}, u32[]{:S(2)}, u32[]{:S(2)}) collective-permute-start(bf16[4,16,1,512]{3,1,2,0:T(8,128)(2,1)S(1)} %get-tuple-element.12), channel_id=1, source_target_pairs={{1,0},{2,1},{3,2},{4,3},{5,4},{6,5},{7,6},{8,7},{9,8},{10,9},{11,1... | collective-permute-start | bytes 196616 | tf_op jit(solution)/shard_map/ppermute | solution.py:24
Sparse Core Ops, SparseCore 0:
  9.5 113.2 all-gather.1
where the time goes:
time: 174 us; the launch traced here: 173 us
  waiting for transfers between devices  61.7 us (35%)
  blocking collectives  47.5 us (27%)
  matrix products  42.6 us (24%)
  between operations  13.5 us (8%)
  other arithmetic  2.95 us (2%)
  starting transfers between devices  2.59 us (1%)
  local copies, waits for them, and re-layouts  2.48 us (1%)
    all_gather x1, waiting for transfers between devices, shards(): lax.all_gather(conv_weight, 'space', axis=3, tiled=True)  59.1 us
    conv_general_dilated x1, matrix products, shards(): lax.conv_general_dilated(padded[None], lax.all_gather(conv_weight, 'space...  42.6 us
    psum x1, blocking collectives, group_moments(): lax.psum((jnp.sum(grouped, axis=(0, 2)), jnp.sum(grouped * grouped, axis=...  32.3 us
    all_to_all x1, blocking collectives, shards(): lax.all_to_all(layout, 'space', split_axis=1, concat_axis=0, tiled=True)  15.2 us
  transfers between devices with their start and end apart: 3, of which 2 were waited for; matrix products, arithmetic and copies ran while one was open for 3% of the time, Pallas kernels for 0%

commit v1 on v0

v1 whole, which is shorter than its diff:
```python
import jax
import jax.numpy as jnp
from jax import lax
from jax.sharding import PartitionSpec as P

GROUPS = 32
FRAMES = 4
ROWS = 16
EPSILON = 1e-06


def normalised(hidden, gain, shift):
    cells, channels = hidden.shape
    values = hidden.astype(jnp.float32)
    member = (
        jnp.arange(channels)[:, None] // (channels // GROUPS)
        == jnp.arange(channels)[None, :] // (channels // GROUPS)
    ).astype(jnp.float32)
    population = float(cells * (channels // GROUPS))

    def spread_out(v):
        return jnp.dot(v[None], member, precision=lax.Precision.HIGHEST)[0] / population

    average = spread_out(jnp.sum(values, axis=0))
    spread = spread_out(jnp.sum((values - average) ** 2, axis=0))
    scale = lax.rsqrt(spread + EPSILON) * gain
    return jax.nn.silu((values - average) * scale + shift).astype(jnp.bfloat16)


def clamp_shift(x, axis, step):
    length = x.shape[axis]
    if step < 0:
        return jnp.concatenate(
            [lax.slice_in_dim(x, 0, 1, axis=axis), lax.slice_in_dim(x, 0, length - 1, axis=axis)],
            axis=axis,
        )
    return jnp.concatenate(
        [lax.slice_in_dim(x, 1, length, axis=axis), lax.slice_in_dim(x, length - 1, length, axis=axis)],
        axis=axis,
    )


def phases(first, middle, last, axis):
    early = clamp_shift(first, axis, -1) + (middle + last)
    late = (first + middle) + clamp_shift(last, axis, 1)
    return early, late


def shards(hidden, norm_gain, norm_shift, conv_weight, conv_bias):
    devices = lax.axis_size("space")
    channels = hidden.shape[1]
    own = channels // devices
    mine = lax.all_to_all(conv_weight, "space", split_axis=4, concat_axis=3, tiled=True)
    cells = lax.all_gather(hidden, "space", axis=0, tiled=True)
    width = cells.shape[0] // (FRAMES * ROWS)
    active = normalised(cells, norm_gain, norm_shift).reshape(FRAMES, ROWS, width, channels)
    first = active[:1]
    history = jnp.concatenate([first, first, active], axis=0)
    kernel = jnp.transpose(mine, (0, 3, 1, 2, 4)).reshape(3, channels, 9 * own)
    taps = sum(
        lax.dot_general(
            history[a : a + FRAMES].reshape(-1, channels),
            kernel[a],
            (((1,), (0,)), ((), ())),
            preferred_element_type=jnp.float32,
        )
        for a in range(3)
    ).reshape(FRAMES, ROWS, width, 3, 3, own)
    rows = phases(taps[..., 0, :, :], taps[..., 1, :, :], taps[..., 2, :, :], 1)
    cols = [phases(r[..., 0, :], r[..., 1, :], r[..., 2, :], 2) for r in rows]
    result = jnp.stack([jnp.stack(c, axis=3) for c in cols], axis=2)
    result = result.reshape(FRAMES, 2 * ROWS, 2 * width, own)
    bias = lax.dynamic_slice_in_dim(conv_bias, lax.axis_index("space") * own, own)
    decoded = (result + bias.astype(jnp.float32)).astype(jnp.bfloat16)
    return lax.all_to_all(decoded, "space", split_axis=2, concat_axis=3, tiled=True)


def solution(mesh):
    placed = (P(("groups", "space"), None), P(), P(), P(None, None, None, "space", None), P())
    return jax.shard_map(
        shards,
        mesh=mesh,
        in_specs=placed,
        out_specs=P("groups", None, "space", None),
        check_vma=False,
    )
```

time: 174 us -> 171 us (0.983)
  local copies, waits for them, and re-layouts: 2.48 us -> 80.3 us
  matrix products: 42.6 us -> 3.44 us
  waiting for transfers between devices: 61.7 us -> 29 us
  blocking collectives: 47.5 us -> 20.3 us
  other arithmetic: 2.95 us -> 15.6 us
  starting transfers between devices: 2.59 us -> 7.4 us
    all_gather x1, waiting for transfers between devices: 59.1 us -> 0.02 us  [shards(): cells = lax.all_gather(hidden, 'space', axis=0, tiled=True)]
    conv_general_dilated x1 -> x0, matrix products: 42.6 us -> none  [shards(): lax.conv_general_dilated(padded[None], lax.all_gather(conv_weight, 'space...]
    unnamed x2 -> x18, local copies, waits for them, and re-layouts: 0.01 us -> 39.8 us
    psum x1 -> x0, blocking collectives: 32.3 us -> none  [group_moments(): lax.psum((jnp.sum(grouped, axis=(0, 2)), jnp.sum(grouped * grouped, axis=...]
    all_to_all x0 -> x1, waiting for transfers between devices: none -> 28.3 us  [shards(): lax.all_to_all(conv_weight, 'space', split_axis=4, concat_axis=3, tiled=T...]
    all_to_all x0 -> x4, local copies, waits for them, and re-layouts: none -> 16.1 us  [the longest x2 9.35 us: shards(): lax.all_to_all(conv_weight, 'space', split_axis=4, concat_axis=3, tiled=T...]
    slice x3 -> x6, local copies, waits for them, and re-layouts: 0.08 us -> 12.8 us  [the longest x1 7.87 us: shards(): rows = phases(taps[..., 0, :, :], taps[..., 1, :, :], taps[..., 2, :, :], 1)]
    add x0 -> x4, other arithmetic: none -> 9.56 us  [the longest x2 8.96 us: phases(): early = clamp_shift(first, axis, -1) + (middle + last)]
  transfers between devices with their start and end apart: 3 -> 2, of which waited for: 2 -> 1; matrix products, arithmetic and copies ran while one was open for 3% -> 16% of each run, Pallas kernels for 0% -> 0%
where the time goes in v1:
time: 171 us; the launch traced here: 170 us
  local copies, waits for them, and re-layouts  80.3 us (47%)
  waiting for transfers between devices  29 us (17%)
  blocking collectives  20.3 us (12%)
  other arithmetic  15.6 us (9%)
  between operations  13.7 us (8%)
  starting transfers between devices  7.4 us (4%)
  matrix products  3.44 us (2%)
    unnamed x18, local copies, waits for them, and re-layouts  39.8 us
    all_to_all x1, waiting for transfers between devices, shards(): lax.all_to_all(conv_weight, 'space', split_axis=4, concat_axis=3, tiled=T...  28.3 us
    all_to_all x1, blocking collectives, shards(): lax.all_to_all(decoded, 'space', split_axis=2, concat_axis=3, tiled=True)  20.3 us
    all_to_all x2, local copies, waits for them, and re-layouts, shards(): lax.all_to_all(conv_weight, 'space', split_axis=4, concat_axis=3, tiled=T...  9.35 us
    add x2, other arithmetic, phases(): early = clamp_shift(first, axis, -1) + (middle + last)  8.96 us
    slice x1, local copies, waits for them, and re-layouts, shards(): rows = phases(taps[..., 0, :, :], taps[..., 1, :, :], taps[..., 2, :, :], 1)  7.87 us
    all_to_all x1, starting transfers between devices, shards(): lax.all_to_all(conv_weight, 'space', split_axis=4, concat_axis=3, tiled=T...  7.4 us
    all_to_all x2, local copies, waits for them, and re-layouts, shards(): lax.all_to_all(decoded, 'space', split_axis=2, concat_axis=3, tiled=True)  6.76 us
  transfers between devices with their start and end apart: 2, of which 1 were waited for; matrix products, arithmetic and copies ran while one was open for 16% of the time, Pallas kernels for 0%

profile of v1, /device:TPU:0, one launch (start us, length us, event | category | flops | bytes accessed | tf_op | source)
XLA Modules:
  0.0 169.7 jit_solution(7668962532301933557)
XLA Ops:
  7.3 7.4 %copy.38 = bf16[3,3,3,32,512]{3,2,1,0,4:T(4,128)(2,1)} copy(bf16[3,3,3,32,512]{4,3,2,1,0:T(8,128)(2,1)} %param.8) | data formatting | bytes 1769472 | tf_op args[3]
  14.7 7.5 %reshape.129 = bf16[16,2,13824]{2,1,0:T(2,128)(2,1)} reshape(bf16[512,3,3,3,32]{4,3,2,1,0:T(4,128)(2,1)} %bitcast.95) | data formatting | bytes 1769472
  22.2 7.4 %all-to-all-start = ((bf16[16,2,13824]{2,1,0:T(2,128)(2,1)}), bf16[16,2,13824]{2,1,0:T(2,128)(2,1)S(1)}, u32[]{:S(2)}, u32[]{:S(2)}) async-start(bf16[16,2,13824]{2,1,0:T(2,128)(2,1)} %reshape.129), calls=%async_computation | async-start | bytes 1769472 | tf_op jit(solution)/shard_map/all_to_all | solution.py:53
  29.7 28.3 %all-to-all-done = bf16[16,2,13824]{2,1,0:T(2,128)(2,1)S(1)} async-done(((bf16[16,2,13824]{2,1,0:T(2,128)(2,1)}), bf16[16,2,13824]{2,1,0:T(2,128)(2,1)S(1)}, u32[]{:S(2)}, u32[]{:S(2)}) %all-to-all-start) | async-done | bytes 884768 | tf_op jit(solution)/shard_map/all_to_all | solution.py:53
  58.0 5.2 %reshape.130 = bf16[512,3,3,3,32]{4,3,2,1,0:T(4,128)(2,1)} reshape(bf16[16,2,13824]{2,1,0:T(2,128)(2,1)S(1)} %all-to-all-done) | data formatting | bytes 1769472
  63.1 5.2 %copy.60 = bf16[3,3,3,32,16,32]{3,4,5,2,1,0:T(8,128)(2,1)S(1)} copy(bf16[3,3,3,32,16,32]{3,2,1,0,5,4:T(4,128)(2,1)} %bitcast.96) | data formatting | bytes 1769472 | tf_op jit(solution)/shard_map/all_to_all | solution.py:53
  68.4 4.1 %all_to_all.29 = bf16[3,3,3,512,32]{3,4,2,1,0:T(8,128)(2,1)} reshape(bf16[3,3,3,16,32,32]{4,3,5,2,1,0:T(8,128)(2,1)S(1)} %bitcast.100) | data formatting | bytes 1769472 | tf_op jit(solution)/shard_map/all_to_all | solution.py:53
  73.8 2.1 %convert_reduce_fusion = f32[512]{0:T(512)S(1)} fusion(bf16[2048,512]{1,0:T(8,128)(2,1)} %all-gather.2.cloned.1.call-done), kind=kLoop, calls=%fused_computation.1 | loop fusion | flops 2096640 | bytes 2099200 | tf_op jit(solution)/shard_map/reduce_sum | solution.py:24
  81.6 5.2 %reshape.122 = f32[4,16,32,3,3,32]{2,1,0,5,4,3:T(8,128)} reshape(f32[2048,288]{0,1:T(8,128)S(1)} %convolution_add_fusion) | data formatting | bytes 4718592 | tf_op jit(solution)/shard_map/reshape | solution.py:68
  86.9 7.9 %fusion.22 = (f32[4,16,32,1,3,32]{2,1,0,5,4,3:T(8,128)}, f32[4,16,32,1,3,32]{2,1,0,5,4,3:T(8,128)}, f32[4,16,32,1,3,32]{2,1,0,5,4,3:T(8,128)}) fusion(f32[4,16,32,3,3,32]{2,1,0,5,4,3:T(8,128)} %reshape.122), kind=kLoop, calls=%fused_computation.60 | loop fusion | bytes 4718592 | tf_op jit(solution)/shard_map/slice | solution.py:69
  94.8 4.4 %copy.57 = f32[4,16,32,1,3,32]{5,1,0,2,4,3:T(8,128)S(1)} copy(f32[4,16,32,1,3,32]{2,1,0,5,4,3:T(8,128)} %get-tuple-element.7) | data formatting | bytes 1572864
  99.1 2.0 %slice.132 = f32[4,15,32,3,32]{4,1,0,2,3:T(8,128)} slice(f32[4,16,32,3,32]{4,1,0,2,3:T(8,128)S(1)} %bitcast.91), slice={[0:4], [1:16], [0:32], [0:3], [0:32]} | slice | bytes 1474560 | tf_op jit(solution)/shard_map/slice | solution.py:38
  101.3 5.4 %copy.55 = f32[4,16,32,1,3,32]{5,1,0,2,4,3:T(8,128)} copy(f32[4,16,32,1,3,32]{2,1,0,5,4,3:T(8,128)} %get-tuple-element.5) | data formatting | bytes 1572864
  106.7 1.5 slice.121
  108.2 5.4 %copy.56 = f32[4,16,32,1,3,32]{5,1,0,2,4,3:T(8,128)} copy(f32[4,16,32,1,3,32]{2,1,0,5,4,3:T(8,128)} %get-tuple-element.6) | data formatting | bytes 1572864
  113.6 8.2 %maximum_add_fusion = (f32[4,16,32,3,32]{4,1,0,2,3:T(8,128)}, f32[4,16,32,3,32]{4,1,0,2,3:T(8,128)S(1)}) fusion(f32[4,15,32,3,32]{4,1,0,2,3:T(8,128)} %bitcast.94, f32[4,1,32,3,32]{4,1,0,2,3:T(1,128)S(1)} %slice.121, f32[4,16,32,1,3,32]{5,1,0,2,4,3:T(8,128)} %copy.56, f32[4,16,32,1,3,32]{5,1,0,2,4,3:T(8,128)S(1)} %copy.57, ...), kind=kLoop, calls=%fused_computation.15 | loop fusion | flops 1179648 | bytes 5505024 | tf_op jit(solution)/shard_map/add | solution.py:44
  121.8 1.3 slice_bitcast_fusion.7
  123.4 1.6 copy-done
  127.7 3.2 %copy.47 = f32[4,16,2,32,2,32]{5,4,3,2,1,0:T(2,128)S(1)} copy(f32[4,16,2,32,2,32]{5,1,0,3,4,2:T(8,128)S(1)} %pad_maximum_fusion) | data formatting | bytes 2097152 | tf_op jit(solution)/shard_map/stack | solution.py:71
  131.5 1.4 copy.61
  132.9 2.0 %reshape.131 = bf16[16,2,8192]{2,1,0:T(2,128)(2,1)S(1)} reshape(bf16[64,4,32,32]{3,2,1,0:T(8,128)(2,1)S(1)} %bitcast.101) | data formatting | bytes 1048576
  134.8 20.3 %all_to_all.36 = bf16[16,2,8192]{2,1,0:T(2,128)(2,1)S(1)} all-to-all(bf16[16,2,8192]{2,1,0:T(2,128)(2,1)S(1)} %reshape.131), channel_id=1, replica_groups=mesh['groups'=2,'space'=16] {'space'}, dimensions={0} | all-to-all | bytes 1048576 | tf_op jit(solution)/shard_map/all_to_all | solution.py:75
  156.1 2.7 %copy.53 = bf16[4,32,4,16,32]{4,3,2,1,0:T(8,128)(2,1)} copy(bf16[4,32,4,16,32]{4,1,0,2,3:T(8,128)(2,1)S(1)} %bitcast.102) | data formatting | bytes 1048576 | tf_op jit(solution)/shard_map/all_to_all | solution.py:75
  158.8 4.1 %reshape.128 = bf16[4,32,4,512]{3,2,1,0:T(4,128)(2,1)} reshape(bf16[4,32,4,16,32]{4,3,2,1,0:T(8,128)(2,1)} %copy.53) | data formatting | bytes 1048576 | tf_op jit(solution)/shard_map/all_to_all | solution.py:75
  (44 shorter events, 12.4 us)
Async XLA Ops:
  6.5 67.2 %all-gather.2.cloned.1.call-start = ((), (), s32[]{:S(2)}) async-start(), calls=%async_computation.2 | async-start | bytes 2228224 | tf_op jit(solution)/shard_map/all_gather | solution.py:54
  14.7 14.9 %copy-start.4 = (bf16[512]{0:T(512)(128)(2,1)S(1)}, bf16[512]{0:T(512)(128)(2,1)}, u32[]{:S(2)}) copy-start(bf16[512]{0:T(512)(128)(2,1)} %param.9) | copy-start | bytes 3076
  22.2 35.8 %all-to-all-start = ((bf16[16,2,13824]{2,1,0:T(2,128)(2,1)}), bf16[16,2,13824]{2,1,0:T(2,128)(2,1)S(1)}, u32[]{:S(2)}, u32[]{:S(2)}) async-start(bf16[16,2,13824]{2,1,0:T(2,128)(2,1)} %reshape.129), calls=%async_computation | async-start | bytes 1769472 | tf_op jit(solution)/shard_map/all_to_all | solution.py:53
  72.5 4.9 %copy-start.3 = (f32[512]{0:T(512)S(1)}, f32[512]{0:T(512)}, u32[]{:S(2)}) copy-start(f32[512]{0:T(512)} %param.6) | copy-start | bytes 6148
  72.5 4.9 %copy-start.2 = (f32[512]{0:T(512)S(1)}, f32[512]{0:T(512)}, u32[]{:S(2)}) copy-start(f32[512]{0:T(512)} %param.7) | copy-start | bytes 6148
  73.8 2.6 %copy-start.1 = (bf16[2048,512]{1,0:T(8,128)(2,1)S(1)}, bf16[2048,512]{1,0:T(8,128)(2,1)}, u32[]{:S(2)}) copy-start(bf16[2048,512]{1,0:T(8,128)(2,1)} %all-gather.2.cloned.1.call-done) | copy-start | bytes 6291460
  123.1 1.9 %copy-start = (f32[4,16,32,3,32]{4,1,0,2,3:T(8,128)S(1)}, f32[4,16,32,3,32]{4,1,0,2,3:T(8,128)}, u32[]{:S(2)}) copy-start(f32[4,16,32,3,32]{4,1,0,2,3:T(8,128)} %get-tuple-element.10) | copy-start | bytes 2359300
Sparse Core Ops, SparseCore 0:
  9.5 49.5 all-gather.1

commit v2 on v1

--- a/solution.py
+++ b/solution.py
@@ -1,12 +1,18 @@
+import functools
+
 import jax
 import jax.numpy as jnp
 from jax import lax
+from jax.experimental import pallas as pl
+from jax.experimental.pallas import tpu as pltpu
 from jax.sharding import PartitionSpec as P
 
 GROUPS = 32
 FRAMES = 4
 ROWS = 16
 EPSILON = 1e-06
+LANES = 128
+MESH = pl.DeviceIdType.MESH
 
 
 def normalised(hidden, gain, shift):
@@ -75,10 +81,268 @@
     return lax.all_to_all(decoded, "space", split_axis=2, concat_axis=3, tiled=True)
 
 
+def fused(dims, hid_ref, gain_ref, shift_ref, w_ref, bias_ref, out_ref, acts, active, packed, weights,
+          total, leaving, arrived, final, act_send, act_recv, sis_send, w_send, w_recv, x_send, o_send, o_recv):
+    parts, n, own, tokens, channels, width = dims
+    chips = n // 2
+    g, s = lax.axis_index("groups"), lax.axis_index("space")
+    chip, core = s // 2, s % 2
+    odd = chip % 2
+    place = (1 - odd) * (chip // 2) + odd * (chips - 1 - chip // 2)
+
+    def device_at(p):
+        p = lax.rem(p + 2 * chips, chips)
+        far = p // (chips // 2)
+        return ((1 - far) * 2 * p + far * (2 * (chips - 1 - p) + 1)) * 2 + core
+
+    right, left = device_at(place + 1), device_at(place - 1)
+    sister = chip * 2 + 1 - core
+    sends = s % parts == g
+
+    def remote(source, target, send, recv, device, group=None):
+        return pltpu.make_async_remote_copy(
+            src_ref=source, dst_ref=target, send_sem=send, recv_sem=recv,
+            device_id=(g if group is None else group, device), device_id_type=MESH,
+        )
+
+    barrier = pltpu.get_barrier_semaphore()
+    for k in range(1, n):
+        pl.semaphore_signal(barrier, inc=1, device_id=(g, lax.rem(s + k, n)), device_id_type=MESH)
+    for k in range(1, parts):
+        pl.semaphore_signal(barrier, inc=1, device_id=(lax.rem(g + k, parts), s), device_id_type=MESH)
+
+    @pl.when(sends)
+    def _():
+        @pl.loop(0, 9)
+        def _(ab):
+            rows = [w_ref[3 * ab + e] for e in range(3)]
+            for d in range(n):
+                lanes = [r[:, d * own : (d + 1) * own] for r in rows]
+                block = jnp.concatenate(lanes + [jnp.zeros_like(lanes[0])], axis=1)
+                packed[d, ab] = block
+
+    acts[s] = hid_ref[...]
+    pl.semaphore_wait(barrier, n - 1 + parts - 1)
+
+    pending = []
+
+    def go(copy):
+        copy.start()
+        pending.append(copy)
+
+    to_right, to_left = chips // 2, chips - 1 - chips // 2
+    go(remote(hid_ref, acts.at[s], act_send.at[0, 0], act_recv.at[s], right))
+    go(remote(hid_ref, acts.at[s], act_send.at[1, 0], act_recv.at[s], left))
+    go(remote(hid_ref, acts.at[s], sis_send.at[0], act_recv.at[s], sister))
+
+    outgoing = []
+    for k in range(1, n):
+        d = lax.rem(s + k, n)
+        outgoing.append(remote(packed.at[d], weights.at[s], w_send.at[k], w_recv.at[s], d))
+
+    @pl.when(sends)
+    def _():
+        for copy in outgoing:
+            copy.start()
+        weights[s] = packed[s]
+
+    rounds = n // parts
+
+    def relay(i):
+        source = lax.rem(s // parts + i, rounds) * parts + g
+        incoming = remote(weights.at[source], weights.at[source], x_send.at[i, 0], w_recv.at[source], s)
+        if i == 0:
+            @pl.when(s % parts != g)
+            def _():
+                incoming.wait_recv()
+        else:
+            incoming.wait_recv()
+        for k in range(1, parts):
+            go(remote(weights.at[source], weights.at[source], x_send.at[i, k], w_recv.at[source], s,
+                      lax.rem(g + k, parts)))
+
+    def arrival(source):
+        remote(acts.at[source], acts.at[source], act_send.at[0, 0], act_recv.at[source], sister).wait_recv()
+
+    relayed = 0
+    for k in range(1, to_right + 1):
+        for side, hops, step, onward in ((0, to_right, -k, right), (1, to_left, k, left)):
+            if k > hops:
+                continue
+            source = device_at(place + step)
+            arrival(source)
+            if k < hops:
+                go(remote(acts.at[source], acts.at[source], act_send.at[side, k], act_recv.at[source], onward))
+            go(remote(acts.at[source], acts.at[source], sis_send.at[2 * k - 1 + side], act_recv.at[source], sister))
+        while relayed < rounds * k // (to_right + 1):
+            relay(relayed)
+            relayed += 1
+    for k in range(chips):
+        arrival(k * 2 + 1 - core)
+
+    size = channels // GROUPS
+    population = float(n * tokens * size)
+    lane = lax.broadcasted_iota(jnp.int32, (8, channels), 1)
+
+    def over_group(v):
+        v = jnp.broadcast_to(jnp.sum(v, axis=0, keepdims=True), (8, channels))
+        step = 1
+        while step < size:
+            v = v + jnp.where(lane // step % 2 == 1, pltpu.roll(v, step, 1), pltpu.roll(v, channels - step, 1))
+            step *= 2
+        return v[:1] / population
+
+    def add_rows(term):
+        def body(i, carry):
+            v = term(acts[i].astype(jnp.float32))
+            return carry + jnp.sum(v.reshape(tokens // 8, 8, channels), axis=0)
+        return lax.fori_loop(0, n, body, jnp.zeros((8, channels), jnp.float32))
+
+    average = over_group(add_rows(lambda v: v))
+    spread = over_group(add_rows(lambda v: (v - average) * (v - average)))
+    scale = lax.rsqrt(spread + EPSILON) * gain_ref[...]
+    offset = shift_ref[...]
+
+    @pl.loop(0, n)
+    def _(i):
+        v = (acts[i].astype(jnp.float32) - average) * scale + offset
+        active[i] = (v / (1.0 + jnp.exp(-v))).astype(jnp.bfloat16)
+
+    while relayed < rounds:
+        relay(relayed)
+        relayed += 1
+    for i in range(rounds):
+        for k in range(1, parts):
+            source = i * parts + lax.rem(g + k, parts)
+            remote(weights.at[source], weights.at[source], x_send.at[i, 0], w_recv.at[source], s).wait_recv()
+
+    per = n // FRAMES
+    cells = ROWS * width
+    column = lax.broadcasted_iota(jnp.int32, (cells, LANES), 0) % width
+    lanes = lax.broadcasted_iota(jnp.int32, (cells, LANES), 1)
+    bias = bias_ref[...]
+
+    @pl.loop(0, FRAMES)
+    def _(f):
+        taps = jnp.zeros((cells, 3 * LANES), jnp.float32)
+        for a in range(3):
+            frame = jnp.maximum(f + (a - 2), 0)
+            left_side = active[pl.ds(frame * per, per)].reshape(cells, channels)
+            right_side = jnp.concatenate(
+                [weights[:, 3 * a + b].reshape(channels, LANES) for b in range(3)], axis=1
+            )
+            taps = taps + jnp.dot(left_side, right_side, preferred_element_type=jnp.float32)
+        first, middle, last = (taps[:, b * LANES : (b + 1) * LANES] for b in range(3))
+        above = jnp.concatenate([first[:width], first[:-width]], axis=0)
+        below = jnp.concatenate([last[width:], last[-width:]], axis=0)
+        both = []
+        for r in (above + (middle + last), (first + middle) + below):
+            near = pltpu.roll(r, LANES - own, 1)
+            far = pltpu.roll(r, LANES - 2 * own, 1)
+            back = pltpu.roll(r, own, 1)
+            before = jnp.where(column == 0, r, pltpu.roll(r, 1, 0))
+            after = jnp.where(column == width - 1, near, pltpu.roll(near, cells - 1, 0))
+            both.append(jnp.where(lanes < own, before + near + far, back + r + after))
+        joined = jnp.where(lanes < 2 * own, both[0], pltpu.roll(both[1], 2 * own, 1))
+        total[pl.ds(f * cells, cells)] = joined + bias
+
+    local = width // n
+    for d in range(n):
+        for j in range(local):
+            rows = total[pl.ds(d * local + j, FRAMES * ROWS, stride=width), :]
+            leaving[d, j] = rows.astype(jnp.bfloat16)
+    for k in range(1, n):
+        d = lax.rem(s + k, n)
+        go(remote(leaving.at[d], arrived.at[s], o_send.at[k], o_recv.at[s], d))
+    arrived[s] = leaving[s]
+    for k in range(1, n):
+        source = lax.rem(s + n - k, n)
+        remote(arrived.at[source], arrived.at[source], o_send.at[0], o_recv.at[source], s).wait_recv()
+
+    quarter = lax.broadcasted_iota(jnp.int32, (FRAMES * ROWS, LANES), 1) // own
+    for q in range(n // 4):
+        for j in range(local):
+            pieces = [arrived[4 * q + i, j].astype(jnp.float32) for i in range(4)]
+            for phase in range(4):
+                whole = pieces[phase]
+                for i in range(4):
+                    turned = pieces[i] if i == phase else pltpu.roll(pieces[i], (i - phase) % 4 * own, 1)
+                    whole = turned if i == 0 else jnp.where(quarter == i, turned, whole)
+                pr, pc = phase // 2, phase % 2
+                at = (pr * local + j) * 2 + pc
+                final[q, pl.ds(at, FRAMES * ROWS, stride=4 * local), :] = whole
+    for q in range(n // 4):
+        out_ref[:, q * LANES : (q + 1) * LANES] = final[q].astype(jnp.bfloat16)
+
+    for copy in pending:
+        copy.wait_send()
+
+    @pl.when(sends)
+    def _():
+        for copy in outgoing:
+            copy.wait_send()
+
+
+def fused_shards(hidden, norm_gain, norm_shift, conv_weight, conv_bias):
+    n, parts = lax.axis_size("space"), lax.axis_size("groups")
+    tokens, channels = hidden.shape
+    own = channels // n
+    width = n * tokens // (FRAMES * ROWS)
+    local = width // n
+    bias = lax.dynamic_slice_in_dim(conv_bias, lax.axis_index("space") * own, own)
+    bias = jnp.tile(bias.astype(jnp.float32), 4)[None]
+    rows = FRAMES * 2 * ROWS * 2 * local
+    bf16, f32 = jnp.bfloat16, jnp.float32
+    dma = pltpu.SemaphoreType.DMA
+    rounds = n // parts
+    out = pl.pallas_call(
+        functools.partial(fused, (parts, n, own, tokens, channels, width)),
+        out_shape=jax.ShapeDtypeStruct((rows, channels), bf16),
+        in_specs=[pl.BlockSpec(memory_space=pltpu.VMEM)] * 5,
+        out_specs=pl.BlockSpec(memory_space=pltpu.VMEM),
+        scratch_shapes=[
+            pltpu.VMEM((n, tokens, channels), bf16),
+            pltpu.VMEM((n, tokens, channels), bf16),
+            pltpu.VMEM((n, 9, own, LANES), bf16),
+            pltpu.VMEM((n, 9, own, LANES), bf16),
+            pltpu.VMEM((n * tokens, LANES), f32),
+            pltpu.VMEM((n, local, FRAMES * ROWS, LANES), bf16),
+            pltpu.VMEM((n, local, FRAMES * ROWS, LANES), bf16),
+            pltpu.VMEM((n // 4, rows, LANES), f32),
+            dma((2, n // 4 + 1)),
+            dma((n,)),
+            dma((n,)),
+            dma((n,)),
+            dma((n,)),
+            dma((rounds, parts)),
+            dma((n,)),
+            dma((n,)),
+        ],
+        compiler_params=pltpu.CompilerParams(
+            collective_id=0, has_side_effects=True, vmem_limit_bytes=60 * 1024 * 1024
+        ),
+    )(
+        hidden,
+        norm_gain[None],
+        norm_shift[None],
+        conv_weight.reshape(27, own, channels),
+        bias,
+    )
+    return out.reshape(FRAMES, 2 * ROWS, 2 * local, channels)
+
+
+def pick(hidden, norm_gain, norm_shift, conv_weight, conv_bias):
+    n, parts = lax.axis_size("space"), lax.axis_size("groups")
+    own = hidden.shape[1] // n
+    suits = own * 4 == LANES and n % 4 == 0 and n % parts == 0 and hidden.shape[0] % 16 == 0
+    body = fused_shards if suits else shards
+    return body(hidden, norm_gain, norm_shift, conv_weight, conv_bias)
+
+
 def solution(mesh):
     placed = (P(("groups", "space"), None), P(), P(), P(None, None, None, "space", None), P())
     return jax.shard_map(
-        shards,
+        pick,
         mesh=mesh,
         in_specs=placed,
         out_specs=P("groups", None, "space", None),

time: 171 us -> 65.7 us (0.38)
  the two profiles are of different devices: /device:TPU:0 before, /device:TPU:23 now
where the time goes in v2:
time: 65.7 us; the launch traced here: 65.5 us
  Pallas kernels  62.2 us (95%)
  local copies, waits for them, and re-layouts  3.24 us (5%)
    pallas_call x1, Pallas kernels, fused_shards(): pl.pallas_call(functools.partial(fused, (parts, n, own, tokens, channels,...  62.2 us
    reshape x1, local copies, waits for them, and re-layouts, fused_shards(): return out.reshape(FRAMES, 2 * ROWS, 2 * local, channels)  1.96 us

profile of v2, /device:TPU:23, one launch (start us, length us, event | category | flops | bytes accessed | tf_op | source)
XLA Modules:
  0.0 65.5 jit_solution(12710902782177127336)
XLA Ops:
  0.0 0.0 copy-start
  0.0 0.7 %copy-done = bf16[512]{0:T(512)(128)(2,1)S(1)} copy-done((bf16[512]{0:T(512)(128)(2,1)S(1)}, bf16[512]{0:T(512)(128)(2,1)}, u32[]{:S(2)}) %copy-start) | copy-done | bytes 1048
  0.7 0.1 dynamic-slice_convert_fusion
  0.8 0.6 broadcast_in_dim_tile.3.bias_ref
  1.4 62.2 %shard_map.55 = bf16[512,512]{1,0:T(8,128)(2,1)} custom-call(bf16[128,512]{1,0:T(8,128)(2,1)} %hid_ref.1, f32[1,512]{1,0:T(1,128)} %bitcast.4, f32[1,512]{1,0:T(1,128)} %bitcast.5, bf16[27,32,512]{2,1,0:T(8,128)(2,1)} %bitcast.3, f32[1,128]{1,0:T(1,128)} %broadcast_in_dim_tile.3.bias_ref), custom_call_target="tpu_custom_call" | custom-call | tf_op jit(solution)/shard_map/pallas_call | solution.py:298
  63.6 2.0 %reshape.8 = bf16[4,32,4,512]{3,2,1,0:T(4,128)(2,1)} reshape(bf16[512,512]{1,0:T(8,128)(2,1)} %shard_map.55) | data formatting | bytes 1048576 | tf_op jit(solution)/shard_map/reshape | solution.py:331
  (1 shorter events, 0.0 us)
Async XLA Ops:
  0.0 0.7 %copy-start = (bf16[512]{0:T(512)(128)(2,1)S(1)}, bf16[512]{0:T(512)(128)(2,1)}, u32[]{:S(2)}) copy-start(bf16[512]{0:T(512)(128)(2,1)} %param.9) | copy-start | bytes 3076

commit v3 on v2

--- a/solution.py
+++ b/solution.py
@@ -12,6 +12,7 @@
 ROWS = 16
 EPSILON = 1e-06
 LANES = 128
+PIECES = 2
 MESH = pl.DeviceIdType.MESH
 
 
@@ -82,20 +83,17 @@
 
 
 def fused(dims, hid_ref, gain_ref, shift_ref, w_ref, bias_ref, out_ref, acts, active, packed, weights,
-          total, leaving, arrived, final, act_send, act_recv, sis_send, w_send, w_recv, x_send, o_send, o_recv):
+          total, leaving, arrived, final, act_send, act_recv, w_send, w_recv, x_send, o_send, o_recv):
     parts, n, own, tokens, channels, width = dims
     chips = n // 2
     g, s = lax.axis_index("groups"), lax.axis_index("space")
     chip, core = s // 2, s % 2
-    odd = chip % 2
-    place = (1 - odd) * (chip // 2) + odd * (chips - 1 - chip // 2)
-
-    def device_at(p):
-        p = lax.rem(p + 2 * chips, chips)
-        far = p // (chips // 2)
-        return ((1 - far) * 2 * p + far * (2 * (chips - 1 - p) + 1)) * 2 + core
-
-    right, left = device_at(place + 1), device_at(place - 1)
+    length = chips // 2
+    z, y = chip // 2, chip % 2
+
+    def device_at(z, y):
+        return (z * 2 + y) * 2 + core
+
     sister = chip * 2 + 1 - core
     sends = s % parts == g
 
@@ -113,13 +111,18 @@
 
     @pl.when(sends)
     def _():
-        @pl.loop(0, 9)
-        def _(ab):
-            rows = [w_ref[3 * ab + e] for e in range(3)]
+        @pl.loop(0, 3)
+        def _(a):
+            rows = [w_ref[9 * a + i] for i in range(9)]
             for d in range(n):
                 lanes = [r[:, d * own : (d + 1) * own] for r in rows]
-                block = jnp.concatenate(lanes + [jnp.zeros_like(lanes[0])], axis=1)
-                packed[d, ab] = block
+                packed[d, 2 * a] = jnp.concatenate(lanes[:3] + lanes[6:7], axis=1)
+                packed[d, 2 * a + 1] = jnp.concatenate(lanes[3:6] + lanes[7:8], axis=1)
+
+        rows = [w_ref[9 * a + 8] for a in range(3)]
+        for d in range(n):
+            lanes = [r[:, d * own : (d + 1) * own] for r in rows]
+            packed[d, 6] = jnp.concatenate(lanes + [jnp.zeros_like(lanes[0])], axis=1)
 
     acts[s] = hid_ref[...]
     pl.semaphore_wait(barrier, n - 1 + parts - 1)
@@ -130,10 +133,29 @@
         copy.start()
         pending.append(copy)
 
-    to_right, to_left = chips // 2, chips - 1 - chips // 2
-    go(remote(hid_ref, acts.at[s], act_send.at[0, 0], act_recv.at[s], right))
-    go(remote(hid_ref, acts.at[s], act_send.at[1, 0], act_recv.at[s], left))
-    go(remote(hid_ref, acts.at[s], sis_send.at[0], act_recv.at[s], sister))
+    guarded = []
+
+    def go_if(wanted, copy):
+        @pl.when(wanted)
+        def _():
+            copy.start()
+        guarded.append((wanted, copy))
+
+    chunk = tokens // PIECES
+    across = device_at(z, 1 - y)
+
+    def part(source, h):
+        return acts.at[source, pl.ds(h * chunk, chunk)]
+
+    def give(block, source, h, slot, device):
+        return remote(block, part(source, h), act_send.at[slot, source, h], act_recv.at[source, h], device)
+
+    for h in range(PIECES):
+        block = hid_ref.at[pl.ds(h * chunk, chunk)]
+        go_if(z < length - 1, give(block, s, h, 0, s + 4))
+        go_if(z > 0, give(block, s, h, 1, s - 4))
+        go(give(block, s, h, 2, across))
+        go(give(block, s, h, 3, sister))
 
     outgoing = []
     for k in range(1, n):
@@ -149,7 +171,7 @@
     rounds = n // parts
 
     def relay(i):
-        source = lax.rem(s // parts + i, rounds) * parts + g
+        source = lax.rem(s // parts + rounds - i, rounds) * parts + g
         incoming = remote(weights.at[source], weights.at[source], x_send.at[i, 0], w_recv.at[source], s)
         if i == 0:
             @pl.when(s % parts != g)
@@ -161,24 +183,37 @@
             go(remote(weights.at[source], weights.at[source], x_send.at[i, k], w_recv.at[source], s,
                       lax.rem(g + k, parts)))
 
-    def arrival(source):
-        remote(acts.at[source], acts.at[source], act_send.at[0, 0], act_recv.at[source], sister).wait_recv()
+    def arrival(source, h):
+        give(part(source, h), source, h, 0, s).wait_recv()
 
     relayed = 0
-    for k in range(1, to_right + 1):
-        for side, hops, step, onward in ((0, to_right, -k, right), (1, to_left, k, left)):
-            if k > hops:
-                continue
-            source = device_at(place + step)
-            arrival(source)
-            if k < hops:
-                go(remote(acts.at[source], acts.at[source], act_send.at[side, k], act_recv.at[source], onward))
-            go(remote(acts.at[source], acts.at[source], sis_send.at[2 * k - 1 + side], act_recv.at[source], sister))
-        while relayed < rounds * k // (to_right + 1):
+    for k in range(1, length):
+        for h in range(PIECES):
+            for there, step, more, onward, slot in (
+                (z >= k, -k, z < length - 1, s + 4, 0),
+                (z + k < length, k, z > 0, s - 4, 1),
+            ):
+                source = lax.rem(device_at(z + step, y) + n, n)
+
+                @pl.when(there)
+                def _():
+                    arrival(source, h)
+
+                for wanted, target, line in (
+                    (there & more, onward, slot), (there, across, 2), (there, sister, 3)
+                ):
+                    go_if(wanted, give(part(source, h), source, h, line, target))
+        while relayed < rounds * k // length:
             relay(relayed)
             relayed += 1
+    for k in range(length):
+        source = lax.rem(z + k, length) * 4 + (1 - y) * 2 + core
+        for h in range(PIECES):
+            arrival(source, h)
+            go(give(part(source, h), source, h, 3, sister))
     for k in range(chips):
-        arrival(k * 2 + 1 - core)
+        for h in range(PIECES):
+            arrival(k * 2 + 1 - core, h)
 
     size = channels // GROUPS
     population = float(n * tokens * size)
@@ -216,7 +251,7 @@
             source = i * parts + lax.rem(g + k, parts)
             remote(weights.at[source], weights.at[source], x_send.at[i, 0], w_recv.at[source], s).wait_recv()
 
-    per = n // FRAMES
+    per, local = n // FRAMES, width // n
     cells = ROWS * width
     column = lax.broadcasted_iota(jnp.int32, (cells, LANES), 0) % width
     lanes = lax.broadcasted_iota(jnp.int32, (cells, LANES), 1)
@@ -228,11 +263,20 @@
         for a in range(3):
             frame = jnp.maximum(f + (a - 2), 0)
             left_side = active[pl.ds(frame * per, per)].reshape(cells, channels)
+            corner = weights[:, 6].reshape(channels, LANES)
+            if a < 2:
+                cut = LANES - (2 - a) * own
+                corner = jnp.concatenate([corner[:, cut:], corner[:, :cut]], axis=1)
             right_side = jnp.concatenate(
-                [weights[:, 3 * a + b].reshape(channels, LANES) for b in range(3)], axis=1
+                [weights[:, 2 * a + b].reshape(channels, LANES) for b in range(2)] + [corner], axis=1
             )
             taps = taps + jnp.dot(left_side, right_side, preferred_element_type=jnp.float32)
         first, middle, last = (taps[:, b * LANES : (b + 1) * LANES] for b in range(3))
+        last = jnp.where(
+            lanes < own,
+            pltpu.roll(first, own, 1),
+            jnp.where(lanes < 2 * own, pltpu.roll(middle, 2 * own, 1), last),
+        )
         above = jnp.concatenate([first[:width], first[:-width]], axis=0)
         below = jnp.concatenate([last[width:], last[-width:]], axis=0)
         both = []
@@ -246,36 +290,44 @@
         joined = jnp.where(lanes < 2 * own, both[0], pltpu.roll(both[1], 2 * own, 1))
         total[pl.ds(f * cells, cells)] = joined + bias
 
-    local = width // n
-    for d in range(n):
-        for j in range(local):
-            rows = total[pl.ds(d * local + j, FRAMES * ROWS, stride=width), :]
-            leaving[d, j] = rows.astype(jnp.bfloat16)
-    for k in range(1, n):
-        d = lax.rem(s + k, n)
-        go(remote(leaving.at[d], arrived.at[s], o_send.at[k], o_recv.at[s], d))
-    arrived[s] = leaving[s]
-    for k in range(1, n):
-        source = lax.rem(s + n - k, n)
-        remote(arrived.at[source], arrived.at[source], o_send.at[0], o_recv.at[source], s).wait_recv()
-
-    quarter = lax.broadcasted_iota(jnp.int32, (FRAMES * ROWS, LANES), 1) // own
-    for q in range(n // 4):
-        for j in range(local):
-            pieces = [arrived[4 * q + i, j].astype(jnp.float32) for i in range(4)]
-            for phase in range(4):
-                whole = pieces[phase]
-                for i in range(4):
-                    turned = pieces[i] if i == phase else pltpu.roll(pieces[i], (i - phase) % 4 * own, 1)
-                    whole = turned if i == 0 else jnp.where(quarter == i, turned, whole)
-                pr, pc = phase // 2, phase % 2
-                at = (pr * local + j) * 2 + pc
-                final[q, pl.ds(at, FRAMES * ROWS, stride=4 * local), :] = whole
+        for d in range(n):
+            for j in range(local):
+                rows = total[pl.ds(f * cells + d * local + j, ROWS, stride=width), :]
+                leaving[f, d, j] = rows.astype(jnp.bfloat16)
+        for k in range(1, n):
+            d = lax.rem(s + k, n)
+            remote(leaving.at[f, d], arrived.at[f, s], o_send.at[f, k], o_recv.at[f, s], d).start()
+        arrived[f, s] = leaving[f, s]
+
+    quarter = lax.broadcasted_iota(jnp.int32, (ROWS, LANES), 1) // own
+
+    @pl.loop(0, FRAMES)
+    def _(f):
+        for k in range(1, n):
+            source = lax.rem(s + n - k, n)
+            remote(arrived.at[f, source], arrived.at[f, source], o_send.at[f, k], o_recv.at[f, source], s).wait()
+        for q in range(n // 4):
+            for j in range(local):
+                pieces = [arrived[f, 4 * q + i, j].astype(jnp.float32) for i in range(4)]
+                for phase in range(4):
+                    whole = pieces[phase]
+                    for i in range(4):
+                        turned = pieces[i] if i == phase else pltpu.roll(pieces[i], (i - phase) % 4 * own, 1)
+                        whole = turned if i == 0 else jnp.where(quarter == i, turned, whole)
+                    pr, pc = phase // 2, phase % 2
+                    at = f * (ROWS * 4 * local) + (pr * local + j) * 2 + pc
+                    final[q, pl.ds(at, ROWS, stride=4 * local), :] = whole
+
     for q in range(n // 4):
         out_ref[:, q * LANES : (q + 1) * LANES] = final[q].astype(jnp.bfloat16)
 
     for copy in pending:
         copy.wait_send()
+
+    for wanted, copy in guarded:
+        @pl.when(wanted)
+        def _():
+            copy.wait_send()
 
     @pl.when(sends)
     def _():
@@ -303,20 +355,19 @@
         scratch_shapes=[
             pltpu.VMEM((n, tokens, channels), bf16),
             pltpu.VMEM((n, tokens, channels), bf16),
-            pltpu.VMEM((n, 9, own, LANES), bf16),
-            pltpu.VMEM((n, 9, own, LANES), bf16),
+            pltpu.VMEM((n, 7, own, LANES), bf16),
+            pltpu.VMEM((n, 7, own, LANES), bf16),
             pltpu.VMEM((n * tokens, LANES), f32),
-            pltpu.VMEM((n, local, FRAMES * ROWS, LANES), bf16),
-            pltpu.VMEM((n, local, FRAMES * ROWS, LANES), bf16),
+            pltpu.VMEM((FRAMES, n, local, ROWS, LANES), bf16),
+            pltpu.VMEM((FRAMES, n, local, ROWS, LANES), bf16),
             pltpu.VMEM((n // 4, rows, LANES), f32),
-            dma((2, n // 4 + 1)),
-            dma((n,)),
-            dma((n,)),
+            dma((4, n, PIECES)),
+            dma((n, PIECES)),
             dma((n,)),
             dma((n,)),
             dma((rounds, parts)),
-            dma((n,)),
-            dma((n,)),
+            dma((FRAMES, n)),
+            dma((FRAMES, n)),
         ],
         compiler_params=pltpu.CompilerParams(
             collective_id=0, has_side_effects=True, vmem_limit_bytes=60 * 1024 * 1024

time: 65.7 us -> 57.5 us (0.88)
  the two profiles are of different devices: /device:TPU:23 before, /device:TPU:0 now
where the time goes in v3:
time: 57.5 us; the launch traced here: 57.3 us
  Pallas kernels  53.9 us (94%)
  local copies, waits for them, and re-layouts  3.24 us (6%)
    pallas_call x1, Pallas kernels, fused_shards(): pl.pallas_call(functools.partial(fused, (parts, n, own, tokens, channels,...  53.9 us
    reshape x1, local copies, waits for them, and re-layouts, fused_shards(): return out.reshape(FRAMES, 2 * ROWS, 2 * local, channels)  1.96 us

profile of v3, /device:TPU:0, one launch (start us, length us, event | category | flops | bytes accessed | tf_op | source)
XLA Modules:
  0.0 57.3 jit_solution(17751865463273555826)
XLA Ops:
  0.0 0.0 copy-start
  0.0 0.7 %copy-done = bf16[512]{0:T(512)(128)(2,1)S(1)} copy-done((bf16[512]{0:T(512)(128)(2,1)S(1)}, bf16[512]{0:T(512)(128)(2,1)}, u32[]{:S(2)}) %copy-start) | copy-done | bytes 1048
  0.7 0.1 dynamic-slice_convert_fusion
  0.8 0.6 %broadcast_in_dim_tile.3.bias_ref = f32[1,128]{1,0:T(1,128)} reshape(f32[4,32]{1,0:T(4,128)S(1)} %tile.2) | data formatting | bytes 1024 | tf_op jit(solution)/shard_map/broadcast_in_dim;tile | solution.py:345
  1.4 53.9 %shard_map.55 = bf16[512,512]{1,0:T(8,128)(2,1)} custom-call(bf16[128,512]{1,0:T(8,128)(2,1)} %hid_ref.1, f32[1,512]{1,0:T(1,128)} %bitcast.4, f32[1,512]{1,0:T(1,128)} %bitcast.5, bf16[27,32,512]{2,1,0:T(8,128)(2,1)} %bitcast.3, f32[1,128]{1,0:T(1,128)} %broadcast_in_dim_tile.3.bias_ref), custom_call_target="tpu_custom_call" | custom-call | tf_op jit(solution)/shard_map/pallas_call | solution.py:350
  55.3 2.0 %reshape.8 = bf16[4,32,4,512]{3,2,1,0:T(4,128)(2,1)} reshape(bf16[512,512]{1,0:T(8,128)(2,1)} %shard_map.55) | data formatting | bytes 1048576 | tf_op jit(solution)/shard_map/reshape | solution.py:382
  (1 shorter events, 0.0 us)
Async XLA Ops:
  0.0 0.7 %copy-start = (bf16[512]{0:T(512)(128)(2,1)S(1)}, bf16[512]{0:T(512)(128)(2,1)}, u32[]{:S(2)}) copy-start(bf16[512]{0:T(512)(128)(2,1)} %param.9) | copy-start | bytes 3076

commit v4 on v3

--- a/solution.py
+++ b/solution.py
@@ -109,6 +109,39 @@
     for k in range(1, parts):
         pl.semaphore_signal(barrier, inc=1, device_id=(lax.rem(g + k, parts), s), device_id_type=MESH)
 
+    acts[s] = hid_ref[...]
+    pl.semaphore_wait(barrier, n - 1 + parts - 1)
+
+    pending = []
+
+    def go(copy):
+        copy.start()
+        pending.append(copy)
+
+    guarded = []
+
+    def go_if(wanted, copy):
+        @pl.when(wanted)
+        def _():
+            copy.start()
+        guarded.append((wanted, copy))
+
+    chunk = tokens // PIECES
+    across = device_at(z, 1 - y)
+
+    def part(source, h):
+        return acts.at[source, pl.ds(h * chunk, chunk)]
+
+    def give(block, source, h, slot, device):
+        return remote(block, part(source, h), act_send.at[slot, source, h], act_recv.at[source, h], device)
+
+    for h in range(PIECES):
+        block = hid_ref.at[pl.ds(h * chunk, chunk)]
+        go_if(z < length - 1, give(block, s, h, 0, s + 4))
+        go_if(z > 0, give(block, s, h, 1, s - 4))
+        go(give(block, s, h, 2, across))
+        go(give(block, s, h, 3, sister))
+
     @pl.when(sends)
     def _():
         @pl.loop(0, 3)
@@ -123,39 +156,6 @@
         for d in range(n):
             lanes = [r[:, d * own : (d + 1) * own] for r in rows]
             packed[d, 6] = jnp.concatenate(lanes + [jnp.zeros_like(lanes[0])], axis=1)
-
-    acts[s] = hid_ref[...]
-    pl.semaphore_wait(barrier, n - 1 + parts - 1)
-
-    pending = []
-
-    def go(copy):
-        copy.start()
-        pending.append(copy)
-
-    guarded = []
-
-    def go_if(wanted, copy):
-        @pl.when(wanted)
-        def _():
-            copy.start()
-        guarded.append((wanted, copy))
-
-    chunk = tokens // PIECES
-    across = device_at(z, 1 - y)
-
-    def part(source, h):
-        return acts.at[source, pl.ds(h * chunk, chunk)]
-
-    def give(block, source, h, slot, device):
-        return remote(block, part(source, h), act_send.at[slot, source, h], act_recv.at[source, h], device)
-
-    for h in range(PIECES):
-        block = hid_ref.at[pl.ds(h * chunk, chunk)]
-        go_if(z < length - 1, give(block, s, h, 0, s + 4))
-        go_if(z > 0, give(block, s, h, 1, s - 4))
-        go(give(block, s, h, 2, across))
-        go(give(block, s, h, 3, sister))
 
     outgoing = []
     for k in range(1, n):
@@ -203,7 +203,7 @@
                     (there & more, onward, slot), (there, across, 2), (there, sister, 3)
                 ):
                     go_if(wanted, give(part(source, h), source, h, line, target))
-        while relayed < rounds * k // length:
+        while relayed < min(rounds, rounds * (k + 1) // length):
             relay(relayed)
             relayed += 1
     for k in range(length):
@@ -255,7 +255,18 @@
     cells = ROWS * width
     column = lax.broadcasted_iota(jnp.int32, (cells, LANES), 0) % width
     lanes = lax.broadcasted_iota(jnp.int32, (cells, LANES), 1)
-    bias = bias_ref[...]
+    turn = lax.broadcasted_iota(jnp.int32, (8, LANES), 1) // own
+    row = jnp.broadcast_to(bias_ref[...].astype(jnp.float32), (8, channels))
+    held = row[:, :LANES]
+    for q in range(1, n // 4):
+        held = jnp.where(s // 4 == q, row[:, q * LANES : (q + 1) * LANES], held)
+    wide = held
+    for i in range(4):
+        copies = held
+        for j in range(4):
+            copies = jnp.where(turn == j, held if i == j else pltpu.roll(held, (j - i) % 4 * own, 1), copies)
+        wide = jnp.where(s % 4 == i, copies, wide)
+    bias = wide[:1]
 
     @pl.loop(0, FRAMES)
     def _(f):
@@ -341,8 +352,6 @@
     own = channels // n
     width = n * tokens // (FRAMES * ROWS)
     local = width // n
-    bias = lax.dynamic_slice_in_dim(conv_bias, lax.axis_index("space") * own, own)
-    bias = jnp.tile(bias.astype(jnp.float32), 4)[None]
     rows = FRAMES * 2 * ROWS * 2 * local
     bf16, f32 = jnp.bfloat16, jnp.float32
     dma = pltpu.SemaphoreType.DMA
@@ -377,7 +386,7 @@
         norm_gain[None],
         norm_shift[None],
         conv_weight.reshape(27, own, channels),
-        bias,
+        conv_bias[None],
     )
     return out.reshape(FRAMES, 2 * ROWS, 2 * local, channels)
 

time: 57.5 us -> 54.5 us (0.948)
  Pallas kernels: 53.9 us -> 51 us
    pallas_call x1, Pallas kernels: 53.9 us -> 51 us  [fused_shards(): pl.pallas_call(functools.partial(fused, (parts, n, own, tokens, channels,...]
    another operation x2 -> x0, local copies, waits for them, and re-layouts: 0.6 us -> none  [fused_shards(): bias = jnp.tile(bias.astype(jnp.float32), 4)[None]]
    broadcast_in_dim x0 -> x1, local copies, waits for them, and re-layouts: none -> 0.58 us  [fused_shards(): conv_bias[None]]
where the time goes in v4:
time: 54.5 us; the launch traced here: 54.3 us
  Pallas kernels  51 us (94%)
  local copies, waits for them, and re-layouts  3.22 us (6%)
    pallas_call x1, Pallas kernels, fused_shards(): pl.pallas_call(functools.partial(fused, (parts, n, own, tokens, channels,...  51 us
    reshape x1, local copies, waits for them, and re-layouts, fused_shards(): return out.reshape(FRAMES, 2 * ROWS, 2 * local, channels)  1.96 us

profile of v4, /device:TPU:0, one launch (start us, length us, event | category | flops | bytes accessed | tf_op | source)
XLA Modules:
  0.0 54.3 jit_solution(10577820526441235551)
XLA Ops:
  0.0 0.0 copy-start
  0.0 0.7 %copy-done = bf16[512]{0:T(512)(128)(2,1)S(1)} copy-done((bf16[512]{0:T(512)(128)(2,1)S(1)}, bf16[512]{0:T(512)(128)(2,1)}, u32[]{:S(2)}) %copy-start) | copy-done | bytes 1048
  0.7 0.6 %broadcast_in_dim.11.bias_ref = bf16[1,512]{1,0:T(2,128)(2,1)} reshape(bf16[512]{0:T(512)(128)(2,1)S(1)} %copy-done) | data formatting | bytes 2048 | tf_op jit(solution)/shard_map/broadcast_in_dim | solution.py:389
  1.3 51.0 %shard_map.55 = bf16[512,512]{1,0:T(8,128)(2,1)} custom-call(bf16[128,512]{1,0:T(8,128)(2,1)} %hid_ref.1, f32[1,512]{1,0:T(1,128)} %bitcast.4, f32[1,512]{1,0:T(1,128)} %bitcast.5, bf16[27,32,512]{2,1,0:T(8,128)(2,1)} %bitcast.3, bf16[1,512]{1,0:T(2,128)(2,1)} %broadcast_in_dim.11.bias_ref), custom_call_target="tpu_custom_call" | custom-call | tf_op jit(solution)/shard_map/pallas_call | solution.py:359
  52.3 2.0 %reshape.7 = bf16[4,32,4,512]{3,2,1,0:T(4,128)(2,1)} reshape(bf16[512,512]{1,0:T(8,128)(2,1)} %shard_map.55) | data formatting | bytes 1048576 | tf_op jit(solution)/shard_map/reshape | solution.py:391
Async XLA Ops:
  0.0 0.7 %copy-start = (bf16[512]{0:T(512)(128)(2,1)S(1)}, bf16[512]{0:T(512)(128)(2,1)}, u32[]{:S(2)}) copy-start(bf16[512]{0:T(512)(128)(2,1)} %param.9) | copy-start | bytes 3076
